TPU v7x, 32 devices: a whole 2x2x4 slice. The times are simulated.
32 devices in a mesh: grp: 2 (over x), tp: 4 (over y, core), pp: 4 (over z).
Axes of the slice: x: 2, y: 2, z: 4, core: 2. Of those that a mesh axis runs over, the one named last changes fastest.
Arguments:
- tokens: bfloat16 [1024, 8192], P('grp', 'tp'), parts along dimension 0, may hold values from -12 to 12
- gain: bfloat16 [4, 8192], P('pp', 'tp'), may hold values from 0.099609375 to 1.8984375
- q_weight: bfloat16 [4, 8192, 4096], P('pp', None, 'tp'), may hold values from -0.5 to 0.5
- kv_weight: bfloat16 [4, 8192, 2048], P('pp', None, 'tp'), may hold values from -0.5 to 0.5
- out_weight: bfloat16 [4, 4096, 8192], P('pp', None, 'tp'), may hold values from -0.09375 to 0.09375
- page_table: int32 [4, 8, 128], P('pp'), may hold values from 0 to 1023, as said below
- segment_ids: int32 [1024], P('grp'), parts along dimension 0, may hold values from 0 to 2, never falling along the last dimension, each value on 1 to 256 neighbouring positions
Outputs:
- hidden: bfloat16 [1024, 8192], P(('grp', 'pp'), 'tp'), parts along dimension 0
- kv_cache: bfloat16 [4, 2048, 4, 256], P('pp', ('grp', 'tp')), parts along dimension 1
There are 2 independent parts, one for each index of `grp`. A program takes and returns all parts, laid end to end along the dimension named above; an argument that names none is the same for every part. Nothing has to cross between parts.
Inputs may be any that keep to these rules, and one draw needn't show every extreme that they name: `page_table`: every entry of a layer's table is distinct and every one of the 1024 values occurs once. For each layer, head and micro-batch the 16 blocks form a run; in each run half of the devices receive exactly 8 pages and the others none, so each device receives exactly 256 pages of a layer.
All inputs are finite; a program needn't handle non-finite values.
Results may differ from a plain program's by a relative error of at most 0.017.
Values may be sent and summed in bfloat16 or wider, within the bound.
A program may use at most 128 MiB of HBM per device.

v0:
```python
import math
import jax
import jax.numpy as jnp
from jax import lax
from jax.sharding import PartitionSpec as P

MODEL_WIDTH = 8192
HEAD_SIZE = 128
KEY_VALUE_HEADS = 8
MB_TOK = 64
MICRO_BATCHES = 8
PAGE_TOKENS = 4
eps_norm = 1e-05


def partner_2(x, axis, apart):
    return lax.ppermute(x, axis, [(i, i ^ 1 << apart) for i in range(lax.axis_size(axis))])


def shifted(x, axis, by):
    peers = lax.axis_size(axis)
    pairs = [(i, i + by) for i in range(peers) if 0 <= i + by < peers]
    return lax.ppermute(x, axis, pairs)


def from_root(x, axis, root):
    mine = lax.axis_index(axis) == root
    return lax.psum(jnp.where(mine, x, jnp.zeros_like(x)), axis)


def send_pages(kv_own, page_rows, micro_idx, is_live, kv_cache, first_head, tensor_parallel_width):
    row_count = kv_own.shape[0]
    kv_cols = kv_own.shape[1]
    head_width = kv_cache.shape[2]
    cache_page_count = kv_cache.shape[0]
    held_heads = max(1, kv_cols // head_width)
    unit_cols = kv_cols // held_heads
    blocks = row_count // PAGE_TOKENS
    paged_rows = (
        kv_own.reshape(blocks, PAGE_TOKENS, held_heads, unit_cols)
        .transpose(2, 0, 1, 3)
        .reshape(held_heads * blocks, PAGE_TOKENS * unit_cols)
    )
    target_pages = lax.dynamic_slice(
        page_rows, (first_head, micro_idx * blocks), (held_heads, blocks)
    ).reshape(-1)
    device = target_pages // cache_page_count
    cache_page_index = target_pages % cache_page_count
    page_count = held_heads * blocks
    capacity = 2 * page_count // tensor_parallel_width
    onehot = (
        device[:, None] == jnp.arange(tensor_parallel_width, dtype=jnp.int32)[None, :]
    ).astype(jnp.int32)
    earlier = jnp.cumsum(onehot, axis=0) - onehot
    arrival = jnp.sum(earlier * onehot, axis=1)
    position = device * capacity + arrival
    outgoing = (
        jnp.zeros((tensor_parallel_width * capacity, PAGE_TOKENS * unit_cols), jnp.bfloat16)
        .at[position]
        .set(paged_rows)
    )
    labels = (
        jnp.full((tensor_parallel_width * capacity,), cache_page_count, jnp.int32)
        .at[position]
        .set(jnp.where(is_live, cache_page_index, cache_page_count))
    )
    incoming, landing = (
        lax.all_to_all(outgoing, "tp", split_axis=0, concat_axis=0, tiled=True),
        lax.all_to_all(labels, "tp", split_axis=0, concat_axis=0, tiled=True),
    )
    offsets = jnp.arange(tensor_parallel_width, dtype=jnp.int32) * kv_cols % head_width
    lane_ids = jnp.arange(head_width, dtype=jnp.int32)
    within = jnp.arange(unit_cols, dtype=jnp.int32)
    placer = (lane_ids[None, None, :] == offsets[:, None, None] + within[None, :, None]).astype(
        jnp.bfloat16
    )
    spread = jnp.einsum(
        "snw,swv->snv",
        incoming.reshape(tensor_parallel_width, capacity * PAGE_TOKENS, unit_cols),
        placer,
        preferred_element_type=jnp.float32,
    ).astype(jnp.bfloat16)
    return kv_cache.at[landing].add(
        spread.reshape(tensor_parallel_width * capacity, PAGE_TOKENS, head_width), mode="drop"
    )


def body(tokens, gain, q_weight, kv_weight, out_weight, page_table, segment_ids):
    tensor_parallel_width = lax.axis_size("tp")
    pp_size = lax.axis_size("pp")
    tp_rank = lax.axis_index("tp")
    section_idx = lax.axis_index("pp")
    w_query = q_weight[0]
    w_keyval = kv_weight[0]
    w_output = out_weight[0]
    page_rows = page_table[0]
    local_width = tokens.shape[1]
    row_total = tokens.shape[0]
    row_count = MB_TOK
    head_dim = HEAD_SIZE
    kv_cols = w_keyval.shape[1]
    held_heads = max(1, kv_cols // (2 * head_dim))
    q_heads = w_query.shape[1] // head_dim
    per_kv = q_heads // held_heads
    first_head = tp_rank * kv_cols // (2 * head_dim)
    cache_page_count = KEY_VALUE_HEADS * (row_total // PAGE_TOKENS) // tensor_parallel_width
    score_scale = 1.0 / math.sqrt(head_dim)
    step_count = MICRO_BATCHES + pp_size - 1
    key_pos = jnp.arange(row_total, dtype=jnp.int32)

    def add_columns(block_cols):
        return (
            jnp.dot(block_cols, w_query, preferred_element_type=jnp.float32),
            jnp.dot(block_cols, w_keyval, preferred_element_type=jnp.float32),
        )

    def add_outputs(block_cols):
        return jnp.dot(block_cols, w_output, preferred_element_type=jnp.float32)

    def one_step(step_idx, state_tuple):
        received, kv_buffer, kv_cache, collected = state_tuple
        micro_raw = step_idx - section_idx
        is_live = (micro_raw >= 0) & (micro_raw < MICRO_BATCHES)
        micro_idx = jnp.clip(micro_raw, 0, MICRO_BATCHES - 1)
        row_start = micro_idx * row_count
        first_rows = lax.dynamic_slice_in_dim(tokens, row_start, row_count, 0)
        current = jnp.where(section_idx == 0, first_rows, received)
        widened = current.astype(jnp.float32)
        partial_sq = jnp.sum(widened * widened, axis=1, keepdims=True)
        mean_sq = lax.psum(partial_sq, "tp") / MODEL_WIDTH
        normed = (widened * lax.rsqrt(mean_sq + eps_norm) * gain.astype(jnp.float32)).astype(
            jnp.bfloat16
        )
        query_sum, keyval_sum = add_columns(lax.all_gather(normed, "tp", axis=1, tiled=True))
        query_matrix = query_sum.astype(jnp.bfloat16)
        kv_own = keyval_sum.astype(jnp.bfloat16)
        if tensor_parallel_width > KEY_VALUE_HEADS:
            partner = partner_2(kv_own, "tp", 0)
            first_half = tp_rank % 2 == 0
            head_pair = jnp.where(
                first_half,
                jnp.concatenate([kv_own, partner], axis=1),
                jnp.concatenate([partner, kv_own], axis=1),
            )
        else:
            head_pair = kv_own
        kv_cache = send_pages(
            kv_own, page_rows, micro_idx, is_live, kv_cache, first_head, tensor_parallel_width
        )
        refreshed = lax.dynamic_update_slice_in_dim(kv_buffer, head_pair, row_start, 0)
        kv_buffer = jnp.where(is_live, refreshed, kv_buffer)
        kv_view = kv_buffer.reshape(row_total, held_heads, 2, head_dim)
        grouped_queries = query_matrix.reshape(row_count, held_heads, per_kv, head_dim)
        scores = (
            jnp.einsum(
                "qgpd,kgd->gpqk",
                grouped_queries,
                kv_view[:, :, 0],
                preferred_element_type=jnp.float32,
            )
            * score_scale
        )
        query_pos = row_start + jnp.arange(row_count, dtype=jnp.int32)
        seg_query = lax.dynamic_slice_in_dim(segment_ids, row_start, row_count, 0)
        allowed = (key_pos[None, :] <= query_pos[:, None]) & (
            segment_ids[None, :] == seg_query[:, None]
        )
        scores = jnp.where(allowed[None, None], scores, -1e30)
        row_max = jnp.max(scores, axis=-1, keepdims=True)
        raised = jnp.exp(scores - row_max)
        weights = (raised / jnp.sum(raised, axis=-1, keepdims=True)).astype(jnp.bfloat16)
        attended = jnp.einsum(
            "gpqk,kgd->qgpd", weights, kv_view[:, :, 1], preferred_element_type=jnp.float32
        )
        attended = attended.astype(jnp.bfloat16).reshape(row_count, q_heads * head_dim)
        projected = add_outputs(lax.all_gather(attended, "tp", axis=1, tiled=True))
        produced = (widened + projected).astype(jnp.bfloat16)
        placed = lax.dynamic_update_slice_in_dim(collected, produced, row_start, 0)
        collected = jnp.where(is_live & (section_idx == pp_size - 1), placed, collected)
        handed = shifted(produced, "pp", 1)
        return (handed, kv_buffer, kv_cache, collected)

    initial = (
        jnp.zeros((row_count, local_width), jnp.bfloat16),
        jnp.zeros((row_total, held_heads * 2 * head_dim), jnp.bfloat16),
        jnp.zeros((cache_page_count, PAGE_TOKENS, 2 * head_dim), jnp.bfloat16),
        jnp.zeros((row_total, local_width), jnp.bfloat16),
    )
    finished = lax.fori_loop(0, step_count, one_step, initial)
    whole_final = from_root(finished[3], "pp", pp_size - 1)
    share_rows = row_total // pp_size
    hidden = lax.dynamic_slice_in_dim(whole_final, section_idx * share_rows, share_rows, 0)
    return (hidden, finished[2][None])


def solution(mesh):
    placed = (
        P("grp", "tp"),
        P("pp", "tp"),
        P("pp", None, "tp"),
        P("pp", None, "tp"),
        P("pp", None, "tp"),
        P("pp", None, None),
        P("grp"),
    )
    return jax.shard_map(
        body,
        mesh=mesh,
        in_specs=placed,
        out_specs=(P(("grp", "pp"), "tp"), P("pp", ("grp", "tp"), None, None)),
        check_vma=False,
    )
```

profile of v0, /device:TPU:0, one launch (start us, length us, event | category | flops | bytes accessed | tf_op | source)
XLA Modules:
  0.0 928.2 jit_solution(15119671289388943089)
XLA Ops:
  9.8 821.5 %while.22 = (s32[]{:T(128)}, bf16[64,2048]{1,0:T(8,128)(2,1)S(1)}, bf16[512,512]{1,0:T(8,128)(2,1)S(1)}, bf16[256,4,256]{2,1,0:T(4,128)(2,1)S(1)}, bf16[512,2048...) while((s32[]{:T(128)}, bf16[64,2048]{1,0:T(8,128)(2,1)S(1)}, ...), condition=%wide.region_10.11_spmd.clone, body=%wide.region_0.10_spmd.clone.sunk | while | flops 2923866880 | bytes 66799608 | solution.py:189
  11.1 8.4 psum.24
  31.1 6.4 all-gather.2.cloned.1.call-done
  37.5 5.3 dynamic-slice_select_fusion.4
  43.0 8.8 convolution_convert_fusion.6
  54.5 7.2 all_gather.25
  61.6 9.6 %select_dynamic-update-slice_fusion.2 = (bf16[512,2048]{1,0:T(8,128)(2,1)}, bf16[64,2048]{1,0:T(8,128)(2,1)S(1)}) fusion(bf16[512,2048]{1,0:T(8,128)(2,1)} %get-tuple-element.624, s32[]{:T(128)S(6)} %select_n.328, pred[]{:T(512)S(6)} %and.146, bf16[64,4096]{1,0:T(8,128)(2,1)S(1)} %all_gather.25, bf16[4096,2048]{1,0:T(8,128)(2,1)} %get-tuple-element.658, ...), kind=kOutput, calls=%fused_computation.27.clone.1 | convolution fusion | flops 1074266112 | bytes 18350084 | tf_op jit(solution)/shard_map/while/body/eval_jaxpr/dot_general | solution.py:118
  88.7 5.8 psum.24
  106.2 5.6 all-gather.2.cloned.1.call-done
  111.8 5.3 dynamic-slice_select_fusion.4
  117.3 8.8 convolution_convert_fusion.6
  129.2 7.2 all_gather.25
  136.3 9.5 %select_dynamic-update-slice_fusion.2 = (bf16[512,2048]{1,0:T(8,128)(2,1)}, bf16[64,2048]{1,0:T(8,128)(2,1)S(1)}) fusion(bf16[512,2048]{1,0:T(8,128)(2,1)} %get-tuple-element.624, s32[]{:T(128)S(6)} %select_n.328, pred[]{:T(512)S(6)} %and.146, bf16[64,4096]{1,0:T(8,128)(2,1)S(1)} %all_gather.25, bf16[4096,2048]{1,0:T(8,128)(2,1)} %get-tuple-element.658, ...), kind=kOutput, calls=%fused_computation.27.clone.1 | convolution fusion | flops 1074266112 | bytes 18350084 | tf_op jit(solution)/shard_map/while/body/eval_jaxpr/dot_general | solution.py:118
  163.0 5.8 psum.24
  180.5 5.6 all-gather.2.cloned.1.call-done
  186.1 5.3 dynamic-slice_select_fusion.4
  191.6 8.8 convolution_convert_fusion.6
  203.0 7.2 all_gather.25
  210.2 9.5 %select_dynamic-update-slice_fusion.2 = (bf16[512,2048]{1,0:T(8,128)(2,1)}, bf16[64,2048]{1,0:T(8,128)(2,1)S(1)}) fusion(bf16[512,2048]{1,0:T(8,128)(2,1)} %get-tuple-element.624, s32[]{:T(128)S(6)} %select_n.328, pred[]{:T(512)S(6)} %and.146, bf16[64,4096]{1,0:T(8,128)(2,1)S(1)} %all_gather.25, bf16[4096,2048]{1,0:T(8,128)(2,1)} %get-tuple-element.658, ...), kind=kOutput, calls=%fused_computation.27.clone.1 | convolution fusion | flops 1074266112 | bytes 18350084 | tf_op jit(solution)/shard_map/while/body/eval_jaxpr/dot_general | solution.py:118
  237.7 5.8 psum.24
  260.3 5.3 dynamic-slice_select_fusion.4
  265.8 8.8 convolution_convert_fusion.6
  277.6 7.2 all_gather.25
  284.8 9.5 %select_dynamic-update-slice_fusion.2 = (bf16[512,2048]{1,0:T(8,128)(2,1)}, bf16[64,2048]{1,0:T(8,128)(2,1)S(1)}) fusion(bf16[512,2048]{1,0:T(8,128)(2,1)} %get-tuple-element.624, s32[]{:T(128)S(6)} %select_n.328, pred[]{:T(512)S(6)} %and.146, bf16[64,4096]{1,0:T(8,128)(2,1)S(1)} %all_gather.25, bf16[4096,2048]{1,0:T(8,128)(2,1)} %get-tuple-element.658, ...), kind=kOutput, calls=%fused_computation.27.clone.1 | convolution fusion | flops 1074266112 | bytes 18350084 | tf_op jit(solution)/shard_map/while/body/eval_jaxpr/dot_general | solution.py:118
  311.4 5.8 psum.24
  328.9 5.6 all-gather.2.cloned.1.call-done
  334.5 5.3 dynamic-slice_select_fusion.4
  340.0 8.8 convolution_convert_fusion.6
  351.5 7.2 all_gather.25
  358.6 9.5 %select_dynamic-update-slice_fusion.2 = (bf16[512,2048]{1,0:T(8,128)(2,1)}, bf16[64,2048]{1,0:T(8,128)(2,1)S(1)}) fusion(bf16[512,2048]{1,0:T(8,128)(2,1)} %get-tuple-element.624, s32[]{:T(128)S(6)} %select_n.328, pred[]{:T(512)S(6)} %and.146, bf16[64,4096]{1,0:T(8,128)(2,1)S(1)} %all_gather.25, bf16[4096,2048]{1,0:T(8,128)(2,1)} %get-tuple-element.658, ...), kind=kOutput, calls=%fused_computation.27.clone.1 | convolution fusion | flops 1074266112 | bytes 18350084 | tf_op jit(solution)/shard_map/while/body/eval_jaxpr/dot_general | solution.py:118
  386.1 5.8 psum.24
  403.6 5.6 all-gather.2.cloned.1.call-done
  409.2 5.3 dynamic-slice_select_fusion.4
  414.7 8.8 convolution_convert_fusion.6
  426.5 7.2 all_gather.25
  433.7 9.5 %select_dynamic-update-slice_fusion.2 = (bf16[512,2048]{1,0:T(8,128)(2,1)}, bf16[64,2048]{1,0:T(8,128)(2,1)S(1)}) fusion(bf16[512,2048]{1,0:T(8,128)(2,1)} %get-tuple-element.624, s32[]{:T(128)S(6)} %select_n.328, pred[]{:T(512)S(6)} %and.146, bf16[64,4096]{1,0:T(8,128)(2,1)S(1)} %all_gather.25, bf16[4096,2048]{1,0:T(8,128)(2,1)} %get-tuple-element.658, ...), kind=kOutput, calls=%fused_computation.27.clone.1 | convolution fusion | flops 1074266112 | bytes 18350084 | tf_op jit(solution)/shard_map/while/body/eval_jaxpr/dot_general | solution.py:118
  460.4 5.8 psum.24
  477.8 5.6 all-gather.2.cloned.1.call-done
  488.9 8.8 convolution_convert_fusion.6
  500.2 7.2 all_gather.25
  507.4 9.5 %select_dynamic-update-slice_fusion.2 = (bf16[512,2048]{1,0:T(8,128)(2,1)}, bf16[64,2048]{1,0:T(8,128)(2,1)S(1)}) fusion(bf16[512,2048]{1,0:T(8,128)(2,1)} %get-tuple-element.624, s32[]{:T(128)S(6)} %select_n.328, pred[]{:T(512)S(6)} %and.146, bf16[64,4096]{1,0:T(8,128)(2,1)S(1)} %all_gather.25, bf16[4096,2048]{1,0:T(8,128)(2,1)} %get-tuple-element.658, ...), kind=kOutput, calls=%fused_computation.27.clone.1 | convolution fusion | flops 1074266112 | bytes 18350084 | tf_op jit(solution)/shard_map/while/body/eval_jaxpr/dot_general | solution.py:118
  535.0 5.8 psum.24
  552.5 5.5 all-gather.2.cloned.1.call-done
  558.0 5.3 dynamic-slice_select_fusion.4
  563.5 8.8 convolution_convert_fusion.6
  575.3 7.2 all_gather.25
  582.4 9.5 %select_dynamic-update-slice_fusion.2 = (bf16[512,2048]{1,0:T(8,128)(2,1)}, bf16[64,2048]{1,0:T(8,128)(2,1)S(1)}) fusion(bf16[512,2048]{1,0:T(8,128)(2,1)} %get-tuple-element.624, s32[]{:T(128)S(6)} %select_n.328, pred[]{:T(512)S(6)} %and.146, bf16[64,4096]{1,0:T(8,128)(2,1)S(1)} %all_gather.25, bf16[4096,2048]{1,0:T(8,128)(2,1)} %get-tuple-element.658, ...), kind=kOutput, calls=%fused_computation.27.clone.1 | convolution fusion | flops 1074266112 | bytes 18350084 | tf_op jit(solution)/shard_map/while/body/eval_jaxpr/dot_general | solution.py:118
  609.1 5.8 psum.24
  626.5 5.7 all-gather.2.cloned.1.call-done
  632.2 5.3 dynamic-slice_select_fusion.4
  637.7 8.8 convolution_convert_fusion.6
  649.5 7.2 all_gather.25
  656.6 9.5 %select_dynamic-update-slice_fusion.2 = (bf16[512,2048]{1,0:T(8,128)(2,1)}, bf16[64,2048]{1,0:T(8,128)(2,1)S(1)}) fusion(bf16[512,2048]{1,0:T(8,128)(2,1)} %get-tuple-element.624, s32[]{:T(128)S(6)} %select_n.328, pred[]{:T(512)S(6)} %and.146, bf16[64,4096]{1,0:T(8,128)(2,1)S(1)} %all_gather.25, bf16[4096,2048]{1,0:T(8,128)(2,1)} %get-tuple-element.658, ...), kind=kOutput, calls=%fused_computation.27.clone.1 | convolution fusion | flops 1074266112 | bytes 18350084 | tf_op jit(solution)/shard_map/while/body/eval_jaxpr/dot_general | solution.py:118
  683.8 5.8 psum.24
  701.3 5.5 all-gather.2.cloned.1.call-done
  706.8 5.3 dynamic-slice_select_fusion.4
  712.3 8.8 convolution_convert_fusion.6
  724.1 7.2 all_gather.25
  731.2 9.5 %select_dynamic-update-slice_fusion.2 = (bf16[512,2048]{1,0:T(8,128)(2,1)}, bf16[64,2048]{1,0:T(8,128)(2,1)S(1)}) fusion(bf16[512,2048]{1,0:T(8,128)(2,1)} %get-tuple-element.624, s32[]{:T(128)S(6)} %select_n.328, pred[]{:T(512)S(6)} %and.146, bf16[64,4096]{1,0:T(8,128)(2,1)S(1)} %all_gather.25, bf16[4096,2048]{1,0:T(8,128)(2,1)} %get-tuple-element.658, ...), kind=kOutput, calls=%fused_computation.27.clone.1 | convolution fusion | flops 1074266112 | bytes 18350084 | tf_op jit(solution)/shard_map/while/body/eval_jaxpr/dot_general | solution.py:118
  758.4 5.8 psum.24
  786.4 8.8 convolution_convert_fusion.6
  798.2 7.2 all_gather.25
  805.4 9.5 %select_dynamic-update-slice_fusion.2 = (bf16[512,2048]{1,0:T(8,128)(2,1)}, bf16[64,2048]{1,0:T(8,128)(2,1)S(1)}) fusion(bf16[512,2048]{1,0:T(8,128)(2,1)} %get-tuple-element.624, s32[]{:T(128)S(6)} %select_n.328, pred[]{:T(512)S(6)} %and.146, bf16[64,4096]{1,0:T(8,128)(2,1)S(1)} %all_gather.25, bf16[4096,2048]{1,0:T(8,128)(2,1)} %get-tuple-element.658, ...), kind=kOutput, calls=%fused_computation.27.clone.1 | convolution fusion | flops 1074266112 | bytes 18350084 | tf_op jit(solution)/shard_map/while/body/eval_jaxpr/dot_general | solution.py:118
  832.9 86.3 %all-reduce.2.cloned.1.call-done = bf16[512,2048]{1,0:T(8,128)(2,1)} async-done(((bf16[512,2048]{1,0:T(8,128)(2,1)}), bf16[512,2048]{1,0:T(8,128)(2,1)}) %all-reduce.2.cloned.1.call-update) | async-done | bytes 2097168 | tf_op jit(solution)/shard_map/psum | solution.py:28
  (579 shorter events, 378.1 us)
Async XLA Ops:
  8.0 1.8 copy-start.2
  8.0 1.8 copy-start.3
  9.8 27.7 %all-gather.2.cloned.1.call-start = ((), (), s32[]{:S(2)}) async-start(), calls=%async_computation.3 | async-start | bytes 1310720 | tf_op jit(solution)/shard_map/while/body/eval_jaxpr/all_gather | solution.py:134
  23.0 6.9 all-to-all-start
  37.5 5.5 copy-start
  71.2 16.3 %collective-permute-start = (bf16[64,2048]{1,0:T(8,128)(2,1)S(1)}, bf16[64,2048]{1,0:T(8,128)(2,1)S(1)}, u32[]{:S(2)}, u32[]{:S(2)}) collective-permute-start(bf16[64,2048]{1,0:T(8,128)(2,1)S(1)} %get-tuple-element.589), channel_id=1, source_target_pairs={{0,1},{1,2},{2,3},{4,5},{5,6},{6,7},{8,9},{9,10},{10,11},{12,13},{... | collective-permute-start | bytes 786440 | tf_op jit(solution)/shard_map/while/body/eval_jaxpr/ppermute | solution.py:23
  76.0 7.9 all-to-all-start.1
  87.5 24.3 %all-gather.2.cloned.1.call-start = ((), (), s32[]{:S(2)}) async-start(), calls=%async_computation.3 | async-start | bytes 1310720 | tf_op jit(solution)/shard_map/while/body/eval_jaxpr/all_gather | solution.py:134
  98.0 6.9 all-to-all-start
  111.8 5.5 copy-start
  145.9 15.9 %collective-permute-start = (bf16[64,2048]{1,0:T(8,128)(2,1)S(1)}, bf16[64,2048]{1,0:T(8,128)(2,1)S(1)}, u32[]{:S(2)}, u32[]{:S(2)}) collective-permute-start(bf16[64,2048]{1,0:T(8,128)(2,1)S(1)} %get-tuple-element.589), channel_id=1, source_target_pairs={{0,1},{1,2},{2,3},{4,5},{5,6},{6,7},{8,9},{9,10},{10,11},{12,13},{... | collective-permute-start | bytes 786440 | tf_op jit(solution)/shard_map/while/body/eval_jaxpr/ppermute | solution.py:23
  150.3 7.9 all-to-all-start.1
  161.8 24.3 %all-gather.2.cloned.1.call-start = ((), (), s32[]{:S(2)}) async-start(), calls=%async_computation.3 | async-start | bytes 1310720 | tf_op jit(solution)/shard_map/while/body/eval_jaxpr/all_gather | solution.py:134
  172.3 6.9 all-to-all-start
  186.1 5.5 copy-start
  219.7 16.7 %collective-permute-start = (bf16[64,2048]{1,0:T(8,128)(2,1)S(1)}, bf16[64,2048]{1,0:T(8,128)(2,1)S(1)}, u32[]{:S(2)}, u32[]{:S(2)}) collective-permute-start(bf16[64,2048]{1,0:T(8,128)(2,1)S(1)} %get-tuple-element.589), channel_id=1, source_target_pairs={{0,1},{1,2},{2,3},{4,5},{5,6},{6,7},{8,9},{9,10},{10,11},{12,13},{... | collective-permute-start | bytes 786440 | tf_op jit(solution)/shard_map/while/body/eval_jaxpr/ppermute | solution.py:23
  225.0 7.9 all-to-all-start.1
  236.5 23.8 %all-gather.2.cloned.1.call-start = ((), (), s32[]{:S(2)}) async-start(), calls=%async_computation.3 | async-start | bytes 1310720 | tf_op jit(solution)/shard_map/while/body/eval_jaxpr/all_gather | solution.py:134
  247.0 6.9 all-to-all-start
  260.3 5.5 copy-start
  294.3 15.9 %collective-permute-start = (bf16[64,2048]{1,0:T(8,128)(2,1)S(1)}, bf16[64,2048]{1,0:T(8,128)(2,1)S(1)}, u32[]{:S(2)}, u32[]{:S(2)}) collective-permute-start(bf16[64,2048]{1,0:T(8,128)(2,1)S(1)} %get-tuple-element.589), channel_id=1, source_target_pairs={{0,1},{1,2},{2,3},{4,5},{5,6},{6,7},{8,9},{9,10},{10,11},{12,13},{... | collective-permute-start | bytes 786440 | tf_op jit(solution)/shard_map/while/body/eval_jaxpr/ppermute | solution.py:23
  298.8 7.9 all-to-all-start.1
  310.2 24.3 %all-gather.2.cloned.1.call-start = ((), (), s32[]{:S(2)}) async-start(), calls=%async_computation.3 | async-start | bytes 1310720 | tf_op jit(solution)/shard_map/while/body/eval_jaxpr/all_gather | solution.py:134
  320.7 6.9 all-to-all-start
  334.5 5.5 copy-start
  368.2 16.7 %collective-permute-start = (bf16[64,2048]{1,0:T(8,128)(2,1)S(1)}, bf16[64,2048]{1,0:T(8,128)(2,1)S(1)}, u32[]{:S(2)}, u32[]{:S(2)}) collective-permute-start(bf16[64,2048]{1,0:T(8,128)(2,1)S(1)} %get-tuple-element.589), channel_id=1, source_target_pairs={{0,1},{1,2},{2,3},{4,5},{5,6},{6,7},{8,9},{9,10},{10,11},{12,13},{... | collective-permute-start | bytes 786440 | tf_op jit(solution)/shard_map/while/body/eval_jaxpr/ppermute | solution.py:23
  373.4 7.9 all-to-all-start.1
  384.9 24.3 %all-gather.2.cloned.1.call-start = ((), (), s32[]{:S(2)}) async-start(), calls=%async_computation.3 | async-start | bytes 1310720 | tf_op jit(solution)/shard_map/while/body/eval_jaxpr/all_gather | solution.py:134
  395.4 6.9 all-to-all-start
  409.2 5.5 copy-start
  443.2 15.9 %collective-permute-start = (bf16[64,2048]{1,0:T(8,128)(2,1)S(1)}, bf16[64,2048]{1,0:T(8,128)(2,1)S(1)}, u32[]{:S(2)}, u32[]{:S(2)}) collective-permute-start(bf16[64,2048]{1,0:T(8,128)(2,1)S(1)} %get-tuple-element.589), channel_id=1, source_target_pairs={{0,1},{1,2},{2,3},{4,5},{5,6},{6,7},{8,9},{9,10},{10,11},{12,13},{... | collective-permute-start | bytes 786440 | tf_op jit(solution)/shard_map/while/body/eval_jaxpr/ppermute | solution.py:23
  447.7 7.9 all-to-all-start.1
  459.1 24.2 %all-gather.2.cloned.1.call-start = ((), (), s32[]{:S(2)}) async-start(), calls=%async_computation.3 | async-start | bytes 1310720 | tf_op jit(solution)/shard_map/while/body/eval_jaxpr/all_gather | solution.py:134
  469.6 6.9 all-to-all-start
  483.4 5.5 copy-start
  516.9 16.8 %collective-permute-start = (bf16[64,2048]{1,0:T(8,128)(2,1)S(1)}, bf16[64,2048]{1,0:T(8,128)(2,1)S(1)}, u32[]{:S(2)}, u32[]{:S(2)}) collective-permute-start(bf16[64,2048]{1,0:T(8,128)(2,1)S(1)} %get-tuple-element.589), channel_id=1, source_target_pairs={{0,1},{1,2},{2,3},{4,5},{5,6},{6,7},{8,9},{9,10},{10,11},{12,13},{... | collective-permute-start | bytes 786440 | tf_op jit(solution)/shard_map/while/body/eval_jaxpr/ppermute | solution.py:23
  522.3 7.9 all-to-all-start.1
  533.7 24.2 %all-gather.2.cloned.1.call-start = ((), (), s32[]{:S(2)}) async-start(), calls=%async_computation.3 | async-start | bytes 1310720 | tf_op jit(solution)/shard_map/while/body/eval_jaxpr/all_gather | solution.py:134
  544.3 6.9 all-to-all-start
  558.0 5.5 copy-start
  592.0 15.9 %collective-permute-start = (bf16[64,2048]{1,0:T(8,128)(2,1)S(1)}, bf16[64,2048]{1,0:T(8,128)(2,1)S(1)}, u32[]{:S(2)}, u32[]{:S(2)}) collective-permute-start(bf16[64,2048]{1,0:T(8,128)(2,1)S(1)} %get-tuple-element.589), channel_id=1, source_target_pairs={{0,1},{1,2},{2,3},{4,5},{5,6},{6,7},{8,9},{9,10},{10,11},{12,13},{... | collective-permute-start | bytes 786440 | tf_op jit(solution)/shard_map/while/body/eval_jaxpr/ppermute | solution.py:23
  596.4 7.9 all-to-all-start.1
  607.9 24.3 %all-gather.2.cloned.1.call-start = ((), (), s32[]{:S(2)}) async-start(), calls=%async_computation.3 | async-start | bytes 1310720 | tf_op jit(solution)/shard_map/while/body/eval_jaxpr/all_gather | solution.py:134
  618.4 6.9 all-to-all-start
  632.2 5.5 copy-start
  666.2 16.4 %collective-permute-start = (bf16[64,2048]{1,0:T(8,128)(2,1)S(1)}, bf16[64,2048]{1,0:T(8,128)(2,1)S(1)}, u32[]{:S(2)}, u32[]{:S(2)}) collective-permute-start(bf16[64,2048]{1,0:T(8,128)(2,1)S(1)} %get-tuple-element.589), channel_id=1, source_target_pairs={{0,1},{1,2},{2,3},{4,5},{5,6},{6,7},{8,9},{9,10},{10,11},{12,13},{... | collective-permute-start | bytes 786440 | tf_op jit(solution)/shard_map/while/body/eval_jaxpr/ppermute | solution.py:23
  671.0 7.9 all-to-all-start.1
  682.6 24.2 %all-gather.2.cloned.1.call-start = ((), (), s32[]{:S(2)}) async-start(), calls=%async_computation.3 | async-start | bytes 1310720 | tf_op jit(solution)/shard_map/while/body/eval_jaxpr/all_gather | solution.py:134
  693.1 6.9 all-to-all-start
  706.8 5.5 copy-start
  740.8 16.4 %collective-permute-start = (bf16[64,2048]{1,0:T(8,128)(2,1)S(1)}, bf16[64,2048]{1,0:T(8,128)(2,1)S(1)}, u32[]{:S(2)}, u32[]{:S(2)}) collective-permute-start(bf16[64,2048]{1,0:T(8,128)(2,1)S(1)} %get-tuple-element.589), channel_id=1, source_target_pairs={{0,1},{1,2},{2,3},{4,5},{5,6},{6,7},{8,9},{9,10},{10,11},{12,13},{... | collective-permute-start | bytes 786440 | tf_op jit(solution)/shard_map/while/body/eval_jaxpr/ppermute | solution.py:23
  745.6 7.9 all-to-all-start.1
  757.2 23.8 %all-gather.2.cloned.1.call-start = ((), (), s32[]{:S(2)}) async-start(), calls=%async_computation.3 | async-start | bytes 1310720 | tf_op jit(solution)/shard_map/while/body/eval_jaxpr/all_gather | solution.py:134
  767.7 6.9 all-to-all-start
  780.9 5.5 copy-start
  814.9 16.4 %collective-permute-start = (bf16[64,2048]{1,0:T(8,128)(2,1)S(1)}, bf16[64,2048]{1,0:T(8,128)(2,1)S(1)}, u32[]{:S(2)}, u32[]{:S(2)}) collective-permute-start(bf16[64,2048]{1,0:T(8,128)(2,1)S(1)} %get-tuple-element.589), channel_id=1, source_target_pairs={{0,1},{1,2},{2,3},{4,5},{5,6},{6,7},{8,9},{9,10},{10,11},{12,13},{... | collective-permute-start | bytes 786440 | tf_op jit(solution)/shard_map/while/body/eval_jaxpr/ppermute | solution.py:23
  819.8 7.9 all-to-all-start.1
  831.3 1.6 copy-start.1
  831.3 87.9 %all-reduce.2.cloned.1.call-start = ((), (), s32[]{:S(2)}) async-start(), calls=%async_computation.2 | async-start | bytes 4194304 | tf_op jit(solution)/shard_map/psum | solution.py:28
Sparse Core Ops, SparseCore 0:
  20.5 17.0 all-gather.1
  95.5 16.2 all-gather.1
  169.8 16.2 all-gather.1
  244.5 15.7 all-gather.1
  318.2 16.2 all-gather.1
  392.9 16.2 all-gather.1
  467.1 16.2 all-gather.1
  541.8 16.1 all-gather.1
  615.9 16.3 all-gather.1
  690.6 16.1 all-gather.1
  765.1 15.7 all-gather.1
Sparse Core Ops, SparseCore 1:
  834.2 85.0 all-reduce.1
where the time goes:
time: 932 us; the launch traced here: 928 us
  matrix products  285 us (31%)
  waiting for transfers between devices  231 us (25%)
  blocking collectives  145 us (16%)
  starting transfers between devices  110 us (12%)
  other arithmetic  70.3 us (8%)
  local copies, waits for them, and re-layouts  69.7 us (7%)
  between operations  15.2 us (2%)
    dot_general x11, matrix products, add_outputs(): return jnp.dot(block_cols, w_output, preferred_element_type=jnp.float32)  105 us
    dot_general x11, matrix products, add_columns(): jnp.dot(block_cols, w_query, preferred_element_type=jnp.float32)  96.7 us
    psum x1, waiting for transfers between devices, from_root(): return lax.psum(jnp.where(mine, x, jnp.zeros_like(x)), axis)  86.3 us
    all_gather x11, blocking collectives, one_step(): projected = add_outputs(lax.all_gather(attended, 'tp', axis=1, tiled=True))  78.7 us
    psum x11, blocking collectives, one_step(): mean_sq = lax.psum(partial_sq, 'tp') / MODEL_WIDTH  66.2 us
    all_gather x11, waiting for transfers between devices, one_step(): lax.all_gather(normed, 'tp', axis=1, tiled=True)  61.4 us
    dot_general x11, matrix products, add_columns(): jnp.dot(block_cols, w_keyval, preferred_element_type=jnp.float32)  58.8 us
    all_to_all x11, waiting for transfers between devices, send_pages(): lax.all_to_all(outgoing, 'tp', split_axis=0, concat_axis=0, tiled=True)  47.7 us
  transfers between devices with their start and end apart: 45, of which 34 were waited for; matrix products, arithmetic and copies ran while one was open for 10% of the time, Pallas kernels for 0%

commit v1 on v0

--- a/solution.py
+++ b/solution.py
@@ -11,6 +11,12 @@
 MICRO_BATCHES = 8
 PAGE_TOKENS = 4
 eps_norm = 1e-05
+
+
+def add_all(x, axis):
+    pieces = lax.all_gather(x, axis, axis=0, tiled=False)
+    total = pieces.sum(axis=0)
+    return total
 
 
 def partner_2(x, axis, apart):
@@ -127,7 +133,7 @@
         current = jnp.where(section_idx == 0, first_rows, received)
         widened = current.astype(jnp.float32)
         partial_sq = jnp.sum(widened * widened, axis=1, keepdims=True)
-        mean_sq = lax.psum(partial_sq, "tp") / MODEL_WIDTH
+        mean_sq = add_all(partial_sq, "tp") / MODEL_WIDTH
         normed = (widened * lax.rsqrt(mean_sq + eps_norm) * gain.astype(jnp.float32)).astype(
             jnp.bfloat16
         )

time: 932 us -> 949 us (1.018)
  local copies, waits for them, and re-layouts: 69.7 us -> 79.7 us
    psum x11 -> x0, blocking collectives: 66.2 us -> none  [one_step(): mean_sq = lax.psum(partial_sq, 'tp') / MODEL_WIDTH]
    while x0 -> x11, blocking collectives: none -> 65.8 us
where the time goes in v1:
time: 949 us; the launch traced here: 946 us
  matrix products  285 us (30%)
  waiting for transfers between devices  231 us (24%)
  blocking collectives  144 us (15%)
  starting transfers between devices  110 us (12%)
  local copies, waits for them, and re-layouts  79.7 us (8%)
  other arithmetic  70.6 us (7%)
  between operations  15.3 us (2%)
  loops' own time  10.2 us (1%)
    dot_general x11, matrix products, add_outputs(): return jnp.dot(block_cols, w_output, preferred_element_type=jnp.float32)  105 us
    dot_general x11, matrix products, add_columns(): jnp.dot(block_cols, w_query, preferred_element_type=jnp.float32)  96.7 us
    psum x1, waiting for transfers between devices, from_root(): return lax.psum(jnp.where(mine, x, jnp.zeros_like(x)), axis)  86.3 us
    all_gather x11, blocking collectives, one_step(): projected = add_outputs(lax.all_gather(attended, 'tp', axis=1, tiled=True))  78.7 us
    while x11, blocking collectives  65.8 us
    all_gather x11, waiting for transfers between devices, one_step(): lax.all_gather(normed, 'tp', axis=1, tiled=True)  61.4 us
    dot_general x11, matrix products, add_columns(): jnp.dot(block_cols, w_keyval, preferred_element_type=jnp.float32)  58.8 us
    all_to_all x11, waiting for transfers between devices, send_pages(): lax.all_to_all(outgoing, 'tp', split_axis=0, concat_axis=0, tiled=True)  47.7 us
  transfers between devices with their start and end apart: 45, of which 34 were waited for; matrix products, arithmetic and copies ran while one was open for 10% of the time, Pallas kernels for 0%

profile of v1, /device:TPU:0, one launch (start us, length us, event | category | flops | bytes accessed | tf_op | source)
XLA Modules:
  0.0 945.5 jit_solution(11369186242155032917)
XLA Ops:
  9.8 838.7 %while.22 = (s32[]{:T(128)}, bf16[64,2048]{1,0:T(8,128)(2,1)S(1)}, bf16[512,512]{1,0:T(8,128)(2,1)S(1)}, bf16[256,4,256]{2,1,0:T(4,128)(2,1)S(1)}, bf16[512,2048...) while((s32[]{:T(128)}, bf16[64,2048]{1,0:T(8,128)(2,1)S(1)}, ...), condition=%wide.region_10.11_spmd.clone, body=%wide.region_0.10_spmd.clone.sunk | while | flops 2923866880 | bytes 66806104 | solution.py:195
  12.6 8.4 all-reduce.3
  32.7 6.4 all-gather.3.cloned.1.call-done
  39.1 5.3 dynamic-slice_select_fusion.4
  44.6 8.8 convolution_convert_fusion.6
  56.0 7.2 all_gather.35
  63.2 9.6 %select_dynamic-update-slice_fusion.2 = (bf16[512,2048]{1,0:T(8,128)(2,1)}, bf16[64,2048]{1,0:T(8,128)(2,1)S(1)}) fusion(bf16[512,2048]{1,0:T(8,128)(2,1)} %get-tuple-element.644, s32[]{:T(128)S(6)} %select_n.328, pred[]{:T(512)S(6)} %and.146, bf16[64,4096]{1,0:T(8,128)(2,1)S(1)} %all_gather.35, bf16[4096,2048]{1,0:T(8,128)(2,1)} %get-tuple-element.682, ...), kind=kOutput, calls=%fused_computation.27.clone.1 | convolution fusion | flops 1074266112 | bytes 18350084 | tf_op jit(solution)/shard_map/while/body/eval_jaxpr/dot_general | solution.py:124
  91.8 5.8 all-reduce.3
  109.3 5.6 all-gather.3.cloned.1.call-done
  120.4 8.8 convolution_convert_fusion.6
  132.3 7.2 all_gather.35
  139.5 9.5 %select_dynamic-update-slice_fusion.2 = (bf16[512,2048]{1,0:T(8,128)(2,1)}, bf16[64,2048]{1,0:T(8,128)(2,1)S(1)}) fusion(bf16[512,2048]{1,0:T(8,128)(2,1)} %get-tuple-element.644, s32[]{:T(128)S(6)} %select_n.328, pred[]{:T(512)S(6)} %and.146, bf16[64,4096]{1,0:T(8,128)(2,1)S(1)} %all_gather.35, bf16[4096,2048]{1,0:T(8,128)(2,1)} %get-tuple-element.682, ...), kind=kOutput, calls=%fused_computation.27.clone.1 | convolution fusion | flops 1074266112 | bytes 18350084 | tf_op jit(solution)/shard_map/while/body/eval_jaxpr/dot_general | solution.py:124
  167.7 5.7 all-reduce.3
  185.2 5.6 all-gather.3.cloned.1.call-done
  196.3 8.8 convolution_convert_fusion.6
  207.8 7.2 all_gather.35
  214.9 9.5 %select_dynamic-update-slice_fusion.2 = (bf16[512,2048]{1,0:T(8,128)(2,1)}, bf16[64,2048]{1,0:T(8,128)(2,1)S(1)}) fusion(bf16[512,2048]{1,0:T(8,128)(2,1)} %get-tuple-element.644, s32[]{:T(128)S(6)} %select_n.328, pred[]{:T(512)S(6)} %and.146, bf16[64,4096]{1,0:T(8,128)(2,1)S(1)} %all_gather.35, bf16[4096,2048]{1,0:T(8,128)(2,1)} %get-tuple-element.682, ...), kind=kOutput, calls=%fused_computation.27.clone.1 | convolution fusion | flops 1074266112 | bytes 18350084 | tf_op jit(solution)/shard_map/while/body/eval_jaxpr/dot_general | solution.py:124
  243.9 5.7 all-reduce.3
  266.6 5.3 dynamic-slice_select_fusion.4
  272.1 8.8 convolution_convert_fusion.6
  283.9 7.2 all_gather.35
  291.1 9.5 %select_dynamic-update-slice_fusion.2 = (bf16[512,2048]{1,0:T(8,128)(2,1)}, bf16[64,2048]{1,0:T(8,128)(2,1)S(1)}) fusion(bf16[512,2048]{1,0:T(8,128)(2,1)} %get-tuple-element.644, s32[]{:T(128)S(6)} %select_n.328, pred[]{:T(512)S(6)} %and.146, bf16[64,4096]{1,0:T(8,128)(2,1)S(1)} %all_gather.35, bf16[4096,2048]{1,0:T(8,128)(2,1)} %get-tuple-element.682, ...), kind=kOutput, calls=%fused_computation.27.clone.1 | convolution fusion | flops 1074266112 | bytes 18350084 | tf_op jit(solution)/shard_map/while/body/eval_jaxpr/dot_general | solution.py:124
  319.2 5.8 all-reduce.3
  336.8 5.6 all-gather.3.cloned.1.call-done
  342.4 5.3 dynamic-slice_select_fusion.4
  347.9 8.8 convolution_convert_fusion.6
  359.3 7.2 all_gather.35
  366.5 9.5 %select_dynamic-update-slice_fusion.2 = (bf16[512,2048]{1,0:T(8,128)(2,1)}, bf16[64,2048]{1,0:T(8,128)(2,1)S(1)}) fusion(bf16[512,2048]{1,0:T(8,128)(2,1)} %get-tuple-element.644, s32[]{:T(128)S(6)} %select_n.328, pred[]{:T(512)S(6)} %and.146, bf16[64,4096]{1,0:T(8,128)(2,1)S(1)} %all_gather.35, bf16[4096,2048]{1,0:T(8,128)(2,1)} %get-tuple-element.682, ...), kind=kOutput, calls=%fused_computation.27.clone.1 | convolution fusion | flops 1074266112 | bytes 18350084 | tf_op jit(solution)/shard_map/while/body/eval_jaxpr/dot_general | solution.py:124
  395.5 5.7 all-reduce.3
  413.0 5.6 all-gather.3.cloned.1.call-done
  418.6 5.3 dynamic-slice_select_fusion.4
  424.1 8.8 convolution_convert_fusion.6
  435.9 7.2 all_gather.35
  443.1 9.5 %select_dynamic-update-slice_fusion.2 = (bf16[512,2048]{1,0:T(8,128)(2,1)}, bf16[64,2048]{1,0:T(8,128)(2,1)S(1)}) fusion(bf16[512,2048]{1,0:T(8,128)(2,1)} %get-tuple-element.644, s32[]{:T(128)S(6)} %select_n.328, pred[]{:T(512)S(6)} %and.146, bf16[64,4096]{1,0:T(8,128)(2,1)S(1)} %all_gather.35, bf16[4096,2048]{1,0:T(8,128)(2,1)} %get-tuple-element.682, ...), kind=kOutput, calls=%fused_computation.27.clone.1 | convolution fusion | flops 1074266112 | bytes 18350084 | tf_op jit(solution)/shard_map/while/body/eval_jaxpr/dot_general | solution.py:124
  471.3 5.7 all-reduce.3
  488.8 5.6 all-gather.3.cloned.1.call-done
  494.4 5.3 dynamic-slice_select_fusion.4
  499.9 8.8 convolution_convert_fusion.6
  511.2 7.2 all_gather.35
  518.4 9.5 %select_dynamic-update-slice_fusion.2 = (bf16[512,2048]{1,0:T(8,128)(2,1)}, bf16[64,2048]{1,0:T(8,128)(2,1)S(1)}) fusion(bf16[512,2048]{1,0:T(8,128)(2,1)} %get-tuple-element.644, s32[]{:T(128)S(6)} %select_n.328, pred[]{:T(512)S(6)} %and.146, bf16[64,4096]{1,0:T(8,128)(2,1)S(1)} %all_gather.35, bf16[4096,2048]{1,0:T(8,128)(2,1)} %get-tuple-element.682, ...), kind=kOutput, calls=%fused_computation.27.clone.1 | convolution fusion | flops 1074266112 | bytes 18350084 | tf_op jit(solution)/shard_map/while/body/eval_jaxpr/dot_general | solution.py:124
  547.4 5.8 all-reduce.3
  565.0 5.5 all-gather.3.cloned.1.call-done
  570.5 5.3 dynamic-slice_select_fusion.4
  576.0 8.8 convolution_convert_fusion.6
  587.8 7.2 all_gather.35
  595.0 9.5 %select_dynamic-update-slice_fusion.2 = (bf16[512,2048]{1,0:T(8,128)(2,1)}, bf16[64,2048]{1,0:T(8,128)(2,1)S(1)}) fusion(bf16[512,2048]{1,0:T(8,128)(2,1)} %get-tuple-element.644, s32[]{:T(128)S(6)} %select_n.328, pred[]{:T(512)S(6)} %and.146, bf16[64,4096]{1,0:T(8,128)(2,1)S(1)} %all_gather.35, bf16[4096,2048]{1,0:T(8,128)(2,1)} %get-tuple-element.682, ...), kind=kOutput, calls=%fused_computation.27.clone.1 | convolution fusion | flops 1074266112 | bytes 18350084 | tf_op jit(solution)/shard_map/while/body/eval_jaxpr/dot_general | solution.py:124
  623.1 5.7 all-reduce.3
  640.7 5.7 all-gather.3.cloned.1.call-done
  646.3 5.3 dynamic-slice_select_fusion.4
  651.8 8.8 convolution_convert_fusion.6
  663.6 7.2 all_gather.35
  670.8 9.5 %select_dynamic-update-slice_fusion.2 = (bf16[512,2048]{1,0:T(8,128)(2,1)}, bf16[64,2048]{1,0:T(8,128)(2,1)S(1)}) fusion(bf16[512,2048]{1,0:T(8,128)(2,1)} %get-tuple-element.644, s32[]{:T(128)S(6)} %select_n.328, pred[]{:T(512)S(6)} %and.146, bf16[64,4096]{1,0:T(8,128)(2,1)S(1)} %all_gather.35, bf16[4096,2048]{1,0:T(8,128)(2,1)} %get-tuple-element.682, ...), kind=kOutput, calls=%fused_computation.27.clone.1 | convolution fusion | flops 1074266112 | bytes 18350084 | tf_op jit(solution)/shard_map/while/body/eval_jaxpr/dot_general | solution.py:124
  699.4 5.7 all-reduce.3
  717.0 5.5 all-gather.3.cloned.1.call-done
  722.5 5.3 dynamic-slice_select_fusion.4
  728.0 8.8 convolution_convert_fusion.6
  739.8 7.2 all_gather.35
  746.9 9.5 %select_dynamic-update-slice_fusion.2 = (bf16[512,2048]{1,0:T(8,128)(2,1)}, bf16[64,2048]{1,0:T(8,128)(2,1)S(1)}) fusion(bf16[512,2048]{1,0:T(8,128)(2,1)} %get-tuple-element.644, s32[]{:T(128)S(6)} %select_n.328, pred[]{:T(512)S(6)} %and.146, bf16[64,4096]{1,0:T(8,128)(2,1)S(1)} %all_gather.35, bf16[4096,2048]{1,0:T(8,128)(2,1)} %get-tuple-element.682, ...), kind=kOutput, calls=%fused_computation.27.clone.1 | convolution fusion | flops 1074266112 | bytes 18350084 | tf_op jit(solution)/shard_map/while/body/eval_jaxpr/dot_general | solution.py:124
  775.6 5.7 all-reduce.3
  798.2 5.3 dynamic-slice_select_fusion.4
  803.7 8.8 convolution_convert_fusion.6
  815.5 7.2 all_gather.35
  822.7 9.5 %select_dynamic-update-slice_fusion.2 = (bf16[512,2048]{1,0:T(8,128)(2,1)}, bf16[64,2048]{1,0:T(8,128)(2,1)S(1)}) fusion(bf16[512,2048]{1,0:T(8,128)(2,1)} %get-tuple-element.644, s32[]{:T(128)S(6)} %select_n.328, pred[]{:T(512)S(6)} %and.146, bf16[64,4096]{1,0:T(8,128)(2,1)S(1)} %all_gather.35, bf16[4096,2048]{1,0:T(8,128)(2,1)} %get-tuple-element.682, ...), kind=kOutput, calls=%fused_computation.27.clone.1 | convolution fusion | flops 1074266112 | bytes 18350084 | tf_op jit(solution)/shard_map/while/body/eval_jaxpr/dot_general | solution.py:124
  850.2 86.3 %all-reduce.6.cloned.1.call-done = bf16[512,2048]{1,0:T(8,128)(2,1)} async-done(((bf16[512,2048]{1,0:T(8,128)(2,1)}), bf16[512,2048]{1,0:T(8,128)(2,1)}) %all-reduce.6.cloned.1.call-update) | async-done | bytes 2097168 | tf_op jit(solution)/shard_map/psum | solution.py:34
  (636 shorter events, 388.4 us)
Async XLA Ops:
  8.0 1.8 copy-start.4
  8.0 1.8 copy-start.2
  8.0 1.8 copy-start.3
  9.9 29.2 %all-gather.3.cloned.1.call-start = ((), (), s32[]{:S(2)}) async-start(), calls=%async_computation.3 | async-start | bytes 1310720 | tf_op jit(solution)/shard_map/while/body/eval_jaxpr/all_gather | solution.py:140
  24.6 6.9 all-to-all-start
  39.1 5.5 copy-start
  72.8 16.3 %collective-permute-start = (bf16[64,2048]{1,0:T(8,128)(2,1)S(1)}, bf16[64,2048]{1,0:T(8,128)(2,1)S(1)}, u32[]{:S(2)}, u32[]{:S(2)}) collective-permute-start(bf16[64,2048]{1,0:T(8,128)(2,1)S(1)} %get-tuple-element.605), channel_id=1, source_target_pairs={{0,1},{1,2},{2,3},{4,5},{5,6},{6,7},{8,9},{9,10},{10,11},{12,13},{... | collective-permute-start | bytes 786440 | tf_op jit(solution)/shard_map/while/body/eval_jaxpr/ppermute | solution.py:29
  77.6 7.9 all-to-all-start.1
  89.1 25.9 %all-gather.3.cloned.1.call-start = ((), (), s32[]{:S(2)}) async-start(), calls=%async_computation.3 | async-start | bytes 1310720 | tf_op jit(solution)/shard_map/while/body/eval_jaxpr/all_gather | solution.py:140
  101.2 6.9 all-to-all-start
  115.0 5.5 copy-start
  149.0 15.9 %collective-permute-start = (bf16[64,2048]{1,0:T(8,128)(2,1)S(1)}, bf16[64,2048]{1,0:T(8,128)(2,1)S(1)}, u32[]{:S(2)}, u32[]{:S(2)}) collective-permute-start(bf16[64,2048]{1,0:T(8,128)(2,1)S(1)} %get-tuple-element.605), channel_id=1, source_target_pairs={{0,1},{1,2},{2,3},{4,5},{5,6},{6,7},{8,9},{9,10},{10,11},{12,13},{... | collective-permute-start | bytes 786440 | tf_op jit(solution)/shard_map/while/body/eval_jaxpr/ppermute | solution.py:29
  153.5 7.9 all-to-all-start.1
  165.0 25.9 %all-gather.3.cloned.1.call-start = ((), (), s32[]{:S(2)}) async-start(), calls=%async_computation.3 | async-start | bytes 1310720 | tf_op jit(solution)/shard_map/while/body/eval_jaxpr/all_gather | solution.py:140
  177.0 6.9 all-to-all-start
  190.8 5.5 copy-start
  224.4 16.7 %collective-permute-start = (bf16[64,2048]{1,0:T(8,128)(2,1)S(1)}, bf16[64,2048]{1,0:T(8,128)(2,1)S(1)}, u32[]{:S(2)}, u32[]{:S(2)}) collective-permute-start(bf16[64,2048]{1,0:T(8,128)(2,1)S(1)} %get-tuple-element.605), channel_id=1, source_target_pairs={{0,1},{1,2},{2,3},{4,5},{5,6},{6,7},{8,9},{9,10},{10,11},{12,13},{... | collective-permute-start | bytes 786440 | tf_op jit(solution)/shard_map/while/body/eval_jaxpr/ppermute | solution.py:29
  229.7 7.9 all-to-all-start.1
  241.2 25.4 %all-gather.3.cloned.1.call-start = ((), (), s32[]{:S(2)}) async-start(), calls=%async_computation.3 | async-start | bytes 1310720 | tf_op jit(solution)/shard_map/while/body/eval_jaxpr/all_gather | solution.py:140
  253.3 6.9 all-to-all-start
  266.6 5.5 copy-start
  300.6 15.8 %collective-permute-start = (bf16[64,2048]{1,0:T(8,128)(2,1)S(1)}, bf16[64,2048]{1,0:T(8,128)(2,1)S(1)}, u32[]{:S(2)}, u32[]{:S(2)}) collective-permute-start(bf16[64,2048]{1,0:T(8,128)(2,1)S(1)} %get-tuple-element.605), channel_id=1, source_target_pairs={{0,1},{1,2},{2,3},{4,5},{5,6},{6,7},{8,9},{9,10},{10,11},{12,13},{... | collective-permute-start | bytes 786440 | tf_op jit(solution)/shard_map/while/body/eval_jaxpr/ppermute | solution.py:29
  305.0 7.9 all-to-all-start.1
  316.5 25.9 %all-gather.3.cloned.1.call-start = ((), (), s32[]{:S(2)}) async-start(), calls=%async_computation.3 | async-start | bytes 1310720 | tf_op jit(solution)/shard_map/while/body/eval_jaxpr/all_gather | solution.py:140
  328.6 6.9 all-to-all-start
  342.4 5.5 copy-start
  376.0 16.7 %collective-permute-start = (bf16[64,2048]{1,0:T(8,128)(2,1)S(1)}, bf16[64,2048]{1,0:T(8,128)(2,1)S(1)}, u32[]{:S(2)}, u32[]{:S(2)}) collective-permute-start(bf16[64,2048]{1,0:T(8,128)(2,1)S(1)} %get-tuple-element.605), channel_id=1, source_target_pairs={{0,1},{1,2},{2,3},{4,5},{5,6},{6,7},{8,9},{9,10},{10,11},{12,13},{... | collective-permute-start | bytes 786440 | tf_op jit(solution)/shard_map/while/body/eval_jaxpr/ppermute | solution.py:29
  381.3 7.9 all-to-all-start.1
  392.8 25.8 %all-gather.3.cloned.1.call-start = ((), (), s32[]{:S(2)}) async-start(), calls=%async_computation.3 | async-start | bytes 1310720 | tf_op jit(solution)/shard_map/while/body/eval_jaxpr/all_gather | solution.py:140
  404.8 6.9 all-to-all-start
  418.6 5.5 copy-start
  452.6 15.9 %collective-permute-start = (bf16[64,2048]{1,0:T(8,128)(2,1)S(1)}, bf16[64,2048]{1,0:T(8,128)(2,1)S(1)}, u32[]{:S(2)}, u32[]{:S(2)}) collective-permute-start(bf16[64,2048]{1,0:T(8,128)(2,1)S(1)} %get-tuple-element.605), channel_id=1, source_target_pairs={{0,1},{1,2},{2,3},{4,5},{5,6},{6,7},{8,9},{9,10},{10,11},{12,13},{... | collective-permute-start | bytes 786440 | tf_op jit(solution)/shard_map/while/body/eval_jaxpr/ppermute | solution.py:29
  457.1 7.9 all-to-all-start.1
  468.5 25.8 %all-gather.3.cloned.1.call-start = ((), (), s32[]{:S(2)}) async-start(), calls=%async_computation.3 | async-start | bytes 1310720 | tf_op jit(solution)/shard_map/while/body/eval_jaxpr/all_gather | solution.py:140
  480.6 6.9 all-to-all-start
  494.4 5.5 copy-start
  527.9 16.8 %collective-permute-start = (bf16[64,2048]{1,0:T(8,128)(2,1)S(1)}, bf16[64,2048]{1,0:T(8,128)(2,1)S(1)}, u32[]{:S(2)}, u32[]{:S(2)}) collective-permute-start(bf16[64,2048]{1,0:T(8,128)(2,1)S(1)} %get-tuple-element.605), channel_id=1, source_target_pairs={{0,1},{1,2},{2,3},{4,5},{5,6},{6,7},{8,9},{9,10},{10,11},{12,13},{... | collective-permute-start | bytes 786440 | tf_op jit(solution)/shard_map/while/body/eval_jaxpr/ppermute | solution.py:29
  533.3 7.9 all-to-all-start.1
  544.7 25.8 %all-gather.3.cloned.1.call-start = ((), (), s32[]{:S(2)}) async-start(), calls=%async_computation.3 | async-start | bytes 1310720 | tf_op jit(solution)/shard_map/while/body/eval_jaxpr/all_gather | solution.py:140
  556.9 6.9 all-to-all-start
  570.5 5.5 copy-start
  604.5 15.9 %collective-permute-start = (bf16[64,2048]{1,0:T(8,128)(2,1)S(1)}, bf16[64,2048]{1,0:T(8,128)(2,1)S(1)}, u32[]{:S(2)}, u32[]{:S(2)}) collective-permute-start(bf16[64,2048]{1,0:T(8,128)(2,1)S(1)} %get-tuple-element.605), channel_id=1, source_target_pairs={{0,1},{1,2},{2,3},{4,5},{5,6},{6,7},{8,9},{9,10},{10,11},{12,13},{... | collective-permute-start | bytes 786440 | tf_op jit(solution)/shard_map/while/body/eval_jaxpr/ppermute | solution.py:29
  608.9 7.9 all-to-all-start.1
  620.4 25.9 %all-gather.3.cloned.1.call-start = ((), (), s32[]{:S(2)}) async-start(), calls=%async_computation.3 | async-start | bytes 1310720 | tf_op jit(solution)/shard_map/while/body/eval_jaxpr/all_gather | solution.py:140
  632.5 6.9 all-to-all-start
  646.3 5.5 copy-start
  680.3 16.4 %collective-permute-start = (bf16[64,2048]{1,0:T(8,128)(2,1)S(1)}, bf16[64,2048]{1,0:T(8,128)(2,1)S(1)}, u32[]{:S(2)}, u32[]{:S(2)}) collective-permute-start(bf16[64,2048]{1,0:T(8,128)(2,1)S(1)} %get-tuple-element.605), channel_id=1, source_target_pairs={{0,1},{1,2},{2,3},{4,5},{5,6},{6,7},{8,9},{9,10},{10,11},{12,13},{... | collective-permute-start | bytes 786440 | tf_op jit(solution)/shard_map/while/body/eval_jaxpr/ppermute | solution.py:29
  685.2 7.9 all-to-all-start.1
  696.7 25.8 %all-gather.3.cloned.1.call-start = ((), (), s32[]{:S(2)}) async-start(), calls=%async_computation.3 | async-start | bytes 1310720 | tf_op jit(solution)/shard_map/while/body/eval_jaxpr/all_gather | solution.py:140
  708.8 6.9 all-to-all-start
  722.5 5.5 copy-start
  756.5 16.4 %collective-permute-start = (bf16[64,2048]{1,0:T(8,128)(2,1)S(1)}, bf16[64,2048]{1,0:T(8,128)(2,1)S(1)}, u32[]{:S(2)}, u32[]{:S(2)}) collective-permute-start(bf16[64,2048]{1,0:T(8,128)(2,1)S(1)} %get-tuple-element.605), channel_id=1, source_target_pairs={{0,1},{1,2},{2,3},{4,5},{5,6},{6,7},{8,9},{9,10},{10,11},{12,13},{... | collective-permute-start | bytes 786440 | tf_op jit(solution)/shard_map/while/body/eval_jaxpr/ppermute | solution.py:29
  761.3 7.9 all-to-all-start.1
  772.9 25.4 %all-gather.3.cloned.1.call-start = ((), (), s32[]{:S(2)}) async-start(), calls=%async_computation.3 | async-start | bytes 1310720 | tf_op jit(solution)/shard_map/while/body/eval_jaxpr/all_gather | solution.py:140
  784.9 6.9 all-to-all-start
  798.2 5.5 copy-start
  832.2 16.4 %collective-permute-start = (bf16[64,2048]{1,0:T(8,128)(2,1)S(1)}, bf16[64,2048]{1,0:T(8,128)(2,1)S(1)}, u32[]{:S(2)}, u32[]{:S(2)}) collective-permute-start(bf16[64,2048]{1,0:T(8,128)(2,1)S(1)} %get-tuple-element.605), channel_id=1, source_target_pairs={{0,1},{1,2},{2,3},{4,5},{5,6},{6,7},{8,9},{9,10},{10,11},{12,13},{... | collective-permute-start | bytes 786440 | tf_op jit(solution)/shard_map/while/body/eval_jaxpr/ppermute | solution.py:29
  837.0 7.9 all-to-all-start.1
  848.6 1.6 copy-start.1
  848.6 87.9 %all-reduce.6.cloned.1.call-start = ((), (), s32[]{:S(2)}) async-start(), calls=%async_computation.2 | async-start | bytes 4194304 | tf_op jit(solution)/shard_map/psum | solution.py:34
Sparse Core Ops, SparseCore 0:
  22.0 17.0 all-gather.2
  98.6 16.2 all-gather.2
  174.5 16.2 all-gather.2
  250.8 15.7 all-gather.2
  326.1 16.2 all-gather.2
  402.3 16.2 all-gather.2
  478.1 16.2 all-gather.2
  554.3 16.1 all-gather.2
  630.0 16.3 all-gather.2
  706.3 16.1 all-gather.2
  782.4 15.7 all-gather.2
Sparse Core Ops, SparseCore 1:
  851.5 85.0 all-reduce.5
